TPU v7x, 32 devices: a whole 2x2x4 slice. The times are simulated.
32 devices in a mesh: space: 16 (over z, y, x), tm: 2 (over core).
Axes of the slice: x: 2, y: 2, z: 4, core: 2. Of those that a mesh axis runs over, the one named last changes fastest.
Arguments:
- vectors: bfloat16 [2, 64, 2, 12, 2048], P('tm', None, None, None, 'space'), may hold values from -6 to 6
- dilution: int32 [64], replicated, may hold values from 0 to 23
- gamma_ids: int32 [16], replicated, may hold values from 1 to 15
Outputs:
- gram: float32 [2, 1024, 128], P(None, 'space')
- loops: float32 [2, 1024, 2], P(None, 'space')
All inputs are finite; a program needn't handle non-finite values.
Results may differ from a plain program's by a relative error of at most 0.0003.
Values sent between devices are 32-bit elements; how exact they have to be, the bound alone decides.
A program may use at most 64 MiB of HBM per device.

v0:
```python
from functools import partial
import math

import jax
import jax.numpy as jnp
from jax import lax
from jax.sharding import PartitionSpec as P

TDIL = 2


highest = lax.Precision.HIGHEST


def zero_square():
    return [[0, 0, 0, 0] for _ in range(4)]


def pair_product(left, right):
    real_out = zero_square()
    imag_out = zero_square()
    for row in range(4):
        for col in range(4):
            acc_real = 0
            acc_imag = 0
            for mid in range(4):
                acc_real += (
                    left[0][row][mid] * right[0][mid][col] - left[1][row][mid] * right[1][mid][col]
                )
                acc_imag += (
                    left[0][row][mid] * right[1][mid][col] + left[1][row][mid] * right[0][mid][col]
                )
            real_out[row][col] = acc_real
            imag_out[row][col] = acc_imag
    return (real_out, imag_out)


def dirac_tables():
    factors = [
        (zero_square(), [[0, 0, 0, 1], [0, 0, 1, 0], [0, -1, 0, 0], [-1, 0, 0, 0]]),
        ([[0, 0, 0, -1], [0, 0, 1, 0], [0, 1, 0, 0], [-1, 0, 0, 0]], zero_square()),
        (zero_square(), [[0, 0, 1, 0], [0, 0, 0, -1], [-1, 0, 0, 0], [0, 1, 0, 0]]),
        ([[0, 0, 1, 0], [0, 0, 0, 1], [1, 0, 0, 0], [0, 1, 0, 0]], zero_square()),
    ]
    reals = []
    imags = []
    for number in range(16):
        current = ([[1 if a == b else 0 for b in range(4)] for a in range(4)], zero_square())
        for position in range(4):
            if number >> position & 1:
                current = pair_product(current, factors[position])
        reals.append([value for line in current[0] for value in line])
        imags.append([value for line in current[1] for value in line])
    return (reals, imags)


def pick_gammas(gamma_ids):
    table_real, table_imag = dirac_tables()
    choose = (gamma_ids[:, None] == jnp.arange(16, dtype=jnp.int32)[None, :]).astype(jnp.float32)
    gamma_real = jnp.dot(
        choose, jnp.asarray(table_real, dtype=jnp.float32), precision=highest
    ).reshape(-1, 4, 4)
    gamma_imag = jnp.dot(
        choose, jnp.asarray(table_imag, dtype=jnp.float32), precision=highest
    ).reshape(-1, 4, 4)
    return (gamma_real, gamma_imag)


def shards(vectors, dilution, gamma_ids):
    slices, count, halves, comps, sites = vectors.shape
    owners = lax.axis_size("space")
    total_sites = sites * owners
    gram_scale = 1.0 / math.sqrt(48.0 * total_sites)
    loop_scale = 1.0 / math.sqrt(1.0 * total_sites)
    gamma_real, gamma_imag = pick_gammas(gamma_ids)
    spin_pick = ((dilution % 12 // 3)[:, None] == jnp.arange(4, dtype=jnp.int32)[None, :]).astype(
        jnp.float32
    )
    colour_pick = ((dilution % 3)[:, None] == jnp.arange(3, dtype=jnp.int32)[None, :]).astype(
        jnp.float32
    )
    time_class = dilution // 12
    ein = partial(jnp.einsum, precision=highest)
    lowein = partial(jnp.einsum, preferred_element_type=jnp.float32)
    first_slice = lax.axis_index("tm") * slices
    rows_real = ein("gba,ib->gia", gamma_real, spin_pick)
    rows_imag = ein("gba,ib->gia", gamma_imag, spin_pick)

    def one_slice(inputs):
        block, slice_index = inputs
        spinor = block.reshape(count, 2, 4, 3 * sites)
        real_part = spinor[:, 0]
        imag_part = spinor[:, 1]
        pair_real = lowein("iak,jbk->iajb", real_part, real_part) + lowein(
            "iak,jbk->iajb", imag_part, imag_part
        )
        pair_imag = lowein("iak,jbk->iajb", real_part, imag_part) - lowein(
            "iak,jbk->iajb", imag_part, real_part
        )
        gram_real = ein("gab,iajb->gij", gamma_real, pair_real) - ein(
            "gab,iajb->gij", gamma_imag, pair_imag
        )
        gram_imag = ein("gab,iajb->gij", gamma_real, pair_imag) + ein(
            "gab,iajb->gij", gamma_imag, pair_real
        )
        gram = jnp.concatenate([gram_real, gram_imag], axis=2).reshape(-1, 2 * count)
        gram = gram * gram_scale
        site_sums = jnp.sum(block, axis=-1, dtype=jnp.float32).reshape(count, 2, 4, 3)
        picked = ein("ipac,ic->ipa", site_sums, colour_pick)
        loop_real = ein("gia,ia->gi", rows_real, picked[:, 0]) - ein(
            "gia,ia->gi", rows_imag, picked[:, 1]
        )
        loop_imag = ein("gia,ia->gi", rows_real, picked[:, 1]) + ein(
            "gia,ia->gi", rows_imag, picked[:, 0]
        )
        live = (time_class == slice_index % TDIL).astype(jnp.float32)[None, :]
        loops = jnp.stack([loop_real * live, loop_imag * live], axis=-1).reshape(-1, 2) * loop_scale
        return (gram, loops)

    gram_terms, loop_terms = lax.map(
        one_slice, (vectors, first_slice + jnp.arange(slices, dtype=jnp.int32))
    )
    total_rows = gram_terms.shape[1]
    owned = total_rows // owners
    totals = lax.psum((gram_terms, loop_terms), "space")
    start = lax.axis_index("space") * owned
    shares = (
        lax.dynamic_slice_in_dim(totals[0], start, owned, 1),
        lax.dynamic_slice_in_dim(totals[1], start, owned, 1),
    )
    gram, loops = (
        lax.all_gather(shares[0], "tm", axis=0, tiled=True),
        lax.all_gather(shares[1], "tm", axis=0, tiled=True),
    )
    return (gram, loops)


def solution(mesh):
    placed = (P("tm", None, None, None, "space"), P(), P())
    return jax.shard_map(
        shards,
        mesh=mesh,
        in_specs=placed,
        out_specs=(P(None, "space", None), P(None, "space", None)),
        check_vma=False,
    )
```

profile of v0, /device:TPU:1, one launch (start us, length us, event | category | flops | bytes accessed | tf_op | source)
XLA Modules:
  0.0 139.2 jit_solution(7025486430821576834)
XLA Ops:
  7.2 0.0 all-reduce.2.cloned.1.call-start
  7.2 1.1 copy.30
  8.3 0.3 reshape.78
  8.6 0.1 fusion.36
  8.7 0.3 fusion.10
  9.0 0.3 fusion.8
  9.4 0.0 copy-start.1
  9.4 0.0 copy-start.3
  9.4 0.3 convolution_add_fusion
  9.7 0.3 copy-done.1
  10.0 0.1 copy-done.3
  10.1 0.0 copy-start.4
  10.1 0.2 fusion.27
  10.3 0.5 copy-done.4
  10.8 0.2 fusion.28
  11.0 0.3 convolution_subtract_fusion
  11.3 1.1 convolution_bitcast_fusion
  12.4 1.1 convolution_bitcast_fusion.2
  13.5 1.1 fusion.1
  14.6 1.1 fusion
  15.7 0.2 maximum_multiply_fusion
  15.9 1.0 copy.38
  16.9 0.0 copy-start
  16.9 0.0 all-reduce.2.cloned.1.call-update
  16.9 1.0 copy-done
  17.9 0.9 convert_reduce_fusion
  18.8 0.2 copy.39
  19.0 0.0 copy-start.2
  19.0 0.2 copy.50
  19.2 0.5 copy-done.2
  19.7 0.1 fusion.24
  19.8 0.4 fusion.22
  20.2 0.1 fusion.37
  20.3 0.1 copy.79
  20.3 0.1 copy.80
  20.4 0.2 convolution_bitcast_fusion.4
  20.7 0.2 multiply_reduce_fusion.3
  20.9 0.1 stack.13
  21.0 0.1 stack.12
  21.1 36.3 %psum.15 = f32[1,1024,2]{1,2,0:T(2,128)S(1)} all-reduce(f32[1,1024,2]{1,2,0:T(2,128)S(1)} %maximum_multiply_fusion.1), channel_id=1, replica_groups=mesh['space'=16,'tm'=2] {'space'}, use_global_device_ids=true, to_apply=%region_2.3 | all-reduce | flops 2048 | bytes 16384 | tf_op jit(solution)/shard_map/psum | solution.py:125
  57.4 0.1 constant_dynamic-slice_fusion
  57.5 9.3 %all_gather.7 = f32[2,64,2]{1,2,0:T(2,128)S(1)} all-gather(f32[1,64,2]{1,2,0:T(2,128)S(1)} %constant_dynamic-slice_fusion), channel_id=1, replica_groups=mesh['space'=16,'tm'=2] {'tm'}, dimensions={0}, use_global_device_ids=true | all-gather | bytes 1536 | tf_op jit(solution)/shard_map/all_gather | solution.py:133
  66.7 59.5 %all-reduce.2.cloned.1.call-done = f32[1,1024,128]{2,1,0:T(8,128)} async-done(((f32[1,1024,128]{2,1,0:T(8,128)}), f32[1,1024,128]{2,1,0:T(8,128)}) %all-reduce.2.cloned.1.call-update) | async-done | bytes 524304 | tf_op jit(solution)/shard_map/psum | solution.py:125
  126.3 0.8 constant_dynamic-slice_fusion.1
  127.0 4.1 %all_gather.6 = f32[2,64,128]{2,1,0:T(8,128)S(1)} all-gather(f32[1,64,128]{2,1,0:T(8,128)S(1)} %constant_dynamic-slice_fusion.1), channel_id=1, replica_groups=mesh['space'=16,'tm'=2] {'tm'}, dimensions={0}, use_global_device_ids=true | all-gather | bytes 98304 | tf_op jit(solution)/shard_map/all_gather | solution.py:132
  131.2 0.6 copy.131
  131.8 0.6 copy.132
  (4 shorter events, 0.1 us)
Async XLA Ops:
  7.2 119.1 %all-reduce.2.cloned.1.call-start = ((), (), s32[]{:S(2)}) async-start(), calls=%async_computation | async-start | bytes 1048576 | tf_op jit(solution)/shard_map/psum | solution.py:125
  9.4 0.7 copy-start.1
  9.4 0.7 copy-start.3
  10.1 0.7 copy-start.4
  16.9 1.0 copy-start
  19.0 0.7 copy-start.2
Sparse Core Ops, SparseCore 0:
  17.0 109.1 all-reduce.1
where the time goes:
time: 140 us; the launch traced here: 139 us
  waiting for transfers between devices  59.6 us (43%)
  blocking collectives  49.7 us (36%)
  between operations  14.2 us (10%)
  local copies, waits for them, and re-layouts  7.59 us (5%)
  matrix products  6.88 us (5%)
    psum x1, waiting for transfers between devices, shards(): totals = lax.psum((gram_terms, loop_terms), 'space')  59.5 us
    psum x1, blocking collectives, shards(): totals = lax.psum((gram_terms, loop_terms), 'space')  36.3 us
    all_gather x1, blocking collectives, shards(): lax.all_gather(shares[1], 'tm', axis=0, tiled=True)  9.26 us
    unnamed x15, local copies, waits for them, and re-layouts  4.74 us
    all_gather x1, blocking collectives, shards(): lax.all_gather(shares[0], 'tm', axis=0, tiled=True)  4.13 us
  transfers between devices with their start and end apart: 1, of which 1 were waited for; matrix products, arithmetic and copies ran while one was open for 2% of the time, Pallas kernels for 0%

commit v1 on v0

--- a/solution.py
+++ b/solution.py
@@ -4,6 +4,8 @@
 import jax
 import jax.numpy as jnp
 from jax import lax
+from jax.experimental import pallas as pl
+from jax.experimental.pallas import tpu as pltpu
 from jax.sharding import PartitionSpec as P
 
 TDIL = 2
@@ -66,6 +68,252 @@
     return (gamma_real, gamma_imag)
 
 
+MESH = pl.DeviceIdType.MESH
+SPINS = 4
+COLOURS = 3
+COMPS = SPINS * COLOURS
+LANES = 128
+
+
+def gamma_entries():
+    reals, imags = dirac_tables()
+    out = []
+    for re, im in zip(reals, imags):
+        rows = []
+        for a in range(SPINS):
+            (b,) = [b for b in range(SPINS) if re[a * SPINS + b] or im[a * SPINS + b]]
+            rows.append((b, re[a * SPINS + b], im[a * SPINS + b]))
+        anti = any(
+            (rows[b][1], rows[b][2]) != (re_ab, -im_ab) for b, re_ab, im_ab in rows
+        )
+        out.append((anti, rows))
+    return out
+
+
+def kernel(
+    owners, groups, per_owner, gram_scale, loop_scale,
+    ids_ref, dil_ref, vec_ref, gram_ref, loops_ref,
+    raw, wide, stack, pairs, packed, sendbuf, recvbuf, mine, theirs,
+    load_sem, send_sem, recv_sem, swap_send, swap_recv,
+):
+    count = vec_ref.shape[0]
+    half = count // 2
+    space = lax.axis_index("space")
+    time = lax.axis_index("tm")
+    load = pltpu.make_async_copy(vec_ref, raw, load_sem)
+    load.start()
+    barrier = pltpu.get_barrier_semaphore()
+    for step in range(1, owners):
+        pl.semaphore_signal(
+            barrier, inc=1, device_id=(lax.rem(space + step, owners), time), device_id_type=MESH
+        )
+    for step in range(1, groups):
+        pl.semaphore_signal(
+            barrier, inc=1, device_id=(space, lax.rem(time + step, groups)), device_id_type=MESH
+        )
+    load.wait()
+
+    for i in range(count):
+        for p in range(2):
+            at = (2 * i + p) * COMPS
+            wide[at : at + COMPS, :] = raw[i, p].astype(jnp.float32)
+    for a in range(SPINS):
+        for p in range(2):
+            for c in range(COLOURS):
+                rows = wide[pl.ds(p * COMPS + COLOURS * a + c, count, stride=2 * COMPS), :]
+                at = (2 * a + p) * count
+                stack[at : at + count, c * LANES : (c + 1) * LANES] = rows.astype(jnp.bfloat16)
+    everything = stack[...]
+    contract = (((1,), (1,)), ((), ()))
+    pairs[...] = lax.dot_general(
+        everything, everything, contract, preferred_element_type=jnp.float32
+    )
+
+    lane = lax.broadcasted_iota(jnp.int32, (1, 2 * count), 1)
+    left = lane < count
+    turn = jnp.where(left, -1.0, 1.0).astype(jnp.float32)
+    dil = dil_ref[...]
+    dil = jnp.concatenate([dil, dil], axis=1)
+    comp = lax.rem(dil, COMPS)
+    spin = lax.div(comp, COLOURS)
+    colour = lax.rem(comp, COLOURS)
+    live = lax.div(dil, COMPS) == lax.rem(time, TDIL)
+    ones = jnp.ones((8, LANES), jnp.bfloat16)
+    sums = [
+        lax.dot_general(
+            ones, everything[:, c * LANES : (c + 1) * LANES], contract,
+            preferred_element_type=jnp.float32,
+        )
+        for c in range(COLOURS)
+    ]
+    quark = []
+    for a in range(SPINS):
+        got = sums[COLOURS - 1][:, a * LANES : (a + 1) * LANES]
+        for c in range(COLOURS - 1):
+            got = jnp.where(colour == c, sums[c][:, a * LANES : (a + 1) * LANES], got)
+        got = jnp.where(live, got, 0.0)
+        quark.append((got, pltpu.roll(got, count, 1) * turn))
+
+    row = lax.broadcasted_iota(jnp.int32, (half, 2 * count), 0)
+    col = lax.broadcasted_iota(jnp.int32, (half, 2 * count), 1)
+    upper = row <= col
+    lower = row + half > col - count
+    low_lanes = col < count
+
+    def block(a, b):
+        first = pairs[2 * a * count : (2 * a + 1) * count, b * LANES : (b + 1) * LANES]
+        second = pairs[(2 * a + 1) * count : (2 * a + 2) * count, b * LANES : (b + 1) * LANES]
+        return first - turn * pltpu.roll(second, count, 1)
+
+    entries = gamma_entries()
+    for shift in range(SPINS):
+        plain = [block(a, a ^ shift) for a in range(SPINS)]
+        turned = [pltpu.roll(x, count, 1) * turn for x in plain]
+        for number, (anti, rows) in enumerate(entries):
+            if rows[0][0] != shift or number == 0:
+                continue
+            total = None
+            loop = jnp.zeros_like(quark[0][0])
+            for a, (b, re, im) in enumerate(rows):
+                term = quark[b][0] if re else quark[b][1]
+                loop = jnp.where(spin == a, term if re + im > 0 else -term, loop)
+                if anti:
+                    re, im = im, -re
+                term = plain[a] if re else turned[a]
+                if total is None:
+                    total = term if re + im > 0 else -term
+                else:
+                    total = total + term if re + im > 0 else total - term
+            top, bottom = total[:half], total[half:]
+            top = jnp.where(upper, top, pltpu.roll(top, count, 1))
+            bottom = jnp.where(lower, bottom, pltpu.roll(bottom, count, 1))
+            packed[number, 0:half, :] = jnp.where(low_lanes, top, bottom)
+            packed[number, half : half + 1, :] = loop[0:1]
+    for g in range(owners * per_owner):
+        sendbuf[g] = packed[ids_ref[g]]
+
+    pl.semaphore_wait(barrier, owners + groups - 2)
+    copies = []
+    for step in range(1, owners):
+        target = lax.rem(space + step, owners)
+        copy = pltpu.make_async_remote_copy(
+            src_ref=sendbuf.at[pl.ds(target * per_owner, per_owner)],
+            dst_ref=recvbuf.at[step - 1],
+            send_sem=send_sem.at[step - 1],
+            recv_sem=recv_sem.at[step - 1],
+            device_id=(target, time),
+            device_id_type=MESH,
+        )
+        copy.start()
+        copies.append(copy)
+    total = sendbuf[pl.ds(space * per_owner, per_owner)]
+    for step in range(1, owners):
+        copies[step - 1].wait_recv()
+        total = total + recvbuf[step - 1]
+    mine[...] = total
+    swaps = []
+    for step in range(1, groups):
+        swap = pltpu.make_async_remote_copy(
+            src_ref=mine,
+            dst_ref=theirs.at[step - 1],
+            send_sem=swap_send.at[step - 1],
+            recv_sem=swap_recv.at[step - 1],
+            device_id=(space, lax.rem(time + step, groups)),
+            device_id_type=MESH,
+        )
+        swap.start()
+        swaps.append(swap)
+
+    above = lax.broadcasted_iota(jnp.int32, (count, 2 * count), 0)
+    across = lax.broadcasted_iota(jnp.int32, (count, 2 * count), 1)
+    in_real = across < count
+    across = jnp.where(in_real, across, across - count)
+
+    def unpack(summed, when):
+        for k in range(per_owner):
+            part = summed[k, 0:half]
+            swapped = pltpu.roll(part, count, 1)
+            full = jnp.concatenate(
+                [jnp.where(low_lanes, part, swapped), jnp.where(low_lanes, swapped, part)], axis=0
+            )
+            flipped = jnp.concatenate([full, full], axis=0).T[:count]
+            real = jnp.where(above <= across, full, flipped)
+            imag = jnp.where(above > across, full, jnp.where(above < across, -flipped, 0.0))
+            held = jnp.where(in_real, real, imag)
+            number = ids_ref[space * per_owner + k]
+            anti = jnp.bool_(False)
+            for n, (is_anti, _) in enumerate(entries):
+                if is_anti:
+                    anti = anti | (number == n)
+            rotated = pltpu.roll(held, count, 1) * turn
+            out = jnp.where(anti, rotated, held)
+            gram_ref[when, k * count : (k + 1) * count, :] = out * gram_scale
+            loops_ref[when, k : k + 1, :] = summed[k, half : half + 1] * loop_scale
+
+    unpack(total, time)
+    for step in range(1, groups):
+        swaps[step - 1].wait_recv()
+        unpack(theirs[step - 1], lax.rem(time + groups - step, groups))
+    for copy in copies + swaps:
+        copy.wait_send()
+
+
+def packed_shards(vectors, dilution, gamma_ids):
+    slices, count, halves, comps, sites = vectors.shape
+    owners, groups = lax.axis_size("space"), lax.axis_size("tm")
+    numbers = gamma_ids.shape[0]
+    per_owner = numbers // owners
+    total_sites = sites * owners
+    message = (per_owner, count // 2 + 1, 2 * count)
+    gram, loops = pl.pallas_call(
+        partial(
+            kernel, owners, groups, per_owner,
+            1.0 / math.sqrt(48.0 * total_sites), 1.0 / math.sqrt(1.0 * total_sites),
+        ),
+        out_shape=(
+            jax.ShapeDtypeStruct((groups, per_owner * count, 2 * count), jnp.float32),
+            jax.ShapeDtypeStruct((groups, per_owner, 2 * count), jnp.float32),
+        ),
+        in_specs=[
+            pl.BlockSpec(memory_space=pltpu.SMEM),
+            pl.BlockSpec(memory_space=pltpu.VMEM),
+            pl.BlockSpec(memory_space=pl.ANY),
+        ],
+        out_specs=(
+            pl.BlockSpec(memory_space=pltpu.VMEM),
+            pl.BlockSpec(memory_space=pltpu.VMEM),
+        ),
+        scratch_shapes=[
+            pltpu.VMEM((count, halves, comps, sites), jnp.bfloat16),
+            pltpu.VMEM((count * halves * comps, sites), jnp.float32),
+            pltpu.VMEM((SPINS * 2 * count, COLOURS * sites), jnp.bfloat16),
+            pltpu.VMEM((SPINS * 2 * count, SPINS * 2 * count), jnp.float32),
+            pltpu.VMEM((16,) + message[1:], jnp.float32),
+            pltpu.VMEM((numbers,) + message[1:], jnp.float32),
+            pltpu.VMEM((owners - 1,) + message, jnp.float32),
+            pltpu.VMEM(message, jnp.float32),
+            pltpu.VMEM((groups - 1,) + message, jnp.float32),
+            pltpu.SemaphoreType.DMA,
+            pltpu.SemaphoreType.DMA((owners - 1,)),
+            pltpu.SemaphoreType.DMA((owners - 1,)),
+            pltpu.SemaphoreType.DMA((groups - 1,)),
+            pltpu.SemaphoreType.DMA((groups - 1,)),
+        ],
+        compiler_params=pltpu.CompilerParams(collective_id=0, has_side_effects=True),
+    )(gamma_ids, dilution.reshape(1, count), vectors.reshape(count, halves, comps, sites))
+    loops = loops.reshape(groups, per_owner, 2, count).swapaxes(2, 3)
+    return gram, loops.reshape(groups, per_owner * count, 2)
+
+
+def any_shards(vectors, dilution, gamma_ids):
+    slices, count, halves, comps, sites = vectors.shape
+    numbers = gamma_ids.shape[0]
+    whole_blocks = numbers % lax.axis_size("space") == 0
+    if slices == 1 and sites == LANES and 2 * count == LANES and whole_blocks:
+        return packed_shards(vectors, dilution, gamma_ids)
+    return shards(vectors, dilution, gamma_ids)
+
+
 def shards(vectors, dilution, gamma_ids):
     slices, count, halves, comps, sites = vectors.shape
     owners = lax.axis_size("space")
@@ -138,7 +386,7 @@
 def solution(mesh):
     placed = (P("tm", None, None, None, "space"), P(), P())
     return jax.shard_map(
-        shards,
+        any_shards,
         mesh=mesh,
         in_specs=placed,
         out_specs=(P(None, "space", None), P(None, "space", None)),

time: 140 us -> 20.9 us (0.15)
  waiting for transfers between devices: 59.6 us -> 0 us
  blocking collectives: 49.7 us -> 0 us
  Pallas kernels: 0 us -> 14.6 us
  between operations: 14.2 us -> 0.65 us
  matrix products: 6.88 us -> 0 us
  local copies, waits for them, and re-layouts: 7.59 us -> 4.65 us
    psum x1 -> x0, waiting for transfers between devices: 59.5 us -> none  [shards(): totals = lax.psum((gram_terms, loop_terms), 'space')]
    psum x1 -> x0, blocking collectives: 36.3 us -> none  [shards(): totals = lax.psum((gram_terms, loop_terms), 'space')]
    pallas_call x0 -> x1, Pallas kernels: none -> 14.6 us  [packed_shards(): pl.pallas_call(partial(kernel, owners, groups, per_owner, 1.0 / math.sqrt...]
    all_gather x2 -> x0, blocking collectives: 13.4 us -> none  [the longest x1 9.26 us: shards(): lax.all_gather(shares[1], 'tm', axis=0, tiled=True)]
    dot_general x13 -> x0, matrix products: 6.88 us -> none  [the longest x1 1.1 us: one_slice(): ein('gab,iajb->gij', gamma_real, pair_imag)]
    unnamed x15 -> x4, local copies, waits for them, and re-layouts: 4.74 us -> 3.48 us
  transfers between devices with their start and end apart: 1 -> 0, of which waited for: 1 -> 0; matrix products, arithmetic and copies ran while one was open for 2% -> 0% of each run, Pallas kernels for 0% -> 0%
where the time goes in v1:
time: 20.9 us; the launch traced here: 20.6 us
  Pallas kernels  14.6 us (70%)
  local copies, waits for them, and re-layouts  4.65 us (22%)
  other arithmetic  0.66 us (3%)
  between operations  0.65 us (3%)
    pallas_call x1, Pallas kernels, packed_shards(): pl.pallas_call(partial(kernel, owners, groups, per_owner, 1.0 / math.sqrt...  14.6 us
    unnamed x4, local copies, waits for them, and re-layouts  3.48 us
    pallas_call x1, other arithmetic, packed_shards(): pl.pallas_call(partial(kernel, owners, groups, per_owner, 1.0 / math.sqrt...  0.66 us
    reshape x1, local copies, waits for them, and re-layouts, packed_shards(): loops = loops.reshape(groups, per_owner, 2, count).swapaxes(2, 3)  0.66 us
    pallas_call x1, local copies, waits for them, and re-layouts, packed_shards(): pl.pallas_call(partial(kernel, owners, groups, per_owner, 1.0 / math.sqrt...  0.51 us

profile of v1, /device:TPU:1, one launch (start us, length us, event | category | flops | bytes accessed | tf_op | source)
XLA Modules:
  0.0 20.6 jit_solution(12693375183319747756)
XLA Ops:
  0.6 1.9 %copy.7 = bf16[1,64,2,12,128]{4,3,2,1,0:T(8,128)(2,1)} copy(bf16[1,64,2,12,128]{4,2,3,1,0:T(2,128)(2,1)} %param.3) | data formatting | bytes 786432 | tf_op args[0]
  2.5 14.6 %shard_map.50 = (f32[2,64,128]{2,1,0:T(8,128)}, f32[2,1,128]{2,1,0:T(1,128)}) custom-call(s32[16]{0:T(128)} %ids_ref.1, s32[1,64]{1,0:T(1,128)} %bitcast.9, bf16[64,2,12,128]{3,2,1,0:T(8,128)(2,1)} %bitcast.7), custom_call_target="tpu_custom_call" | custom-call | tf_op jit(solution)/shard_map/pallas_call | solution.py:268
  17.1 0.0 copy-start
  17.1 0.5 %broadcast.3 = f32[]{:T(128)} broadcast(f32[]{:T(128)} %constant.4), dimensions={} | broadcast | bytes 8 | tf_op jit(solution)/shard_map/pallas_call | solution.py:268
  17.7 0.1 copy-done
  17.8 0.7 %reduce.3 = f32[2,128]{1,0:T(2,128)S(1)} reduce(f32[2,1,128]{2,1,0:T(1,128)S(1)} %copy-done, f32[]{:T(128)} %broadcast.3), dimensions={1}, to_apply=%get-tuple-element.5.reduce_sub_computation.3 | reduce | bytes 2052 | tf_op jit(solution)/shard_map/pallas_call | solution.py:268
  18.5 0.7 %reshape.18 = f32[2,1,2,64]{3,2,0,1:T(2,128)} reshape(f32[2,128]{1,0:T(2,128)S(1)} %reduce.3) | data formatting | bytes 2048 | tf_op jit(solution)/shard_map/reshape | solution.py:304
  19.1 1.5 %copy.9 = f32[2,64,128]{2,1,0:T(8,128)} copy(f32[2,64,128]{2,1,0:T(8,128)} %get-tuple-element.8) | data formatting | bytes 131072
Async XLA Ops:
  17.1 0.7 %copy-start = (f32[2,1,128]{2,1,0:T(1,128)S(1)}, f32[2,1,128]{2,1,0:T(1,128)}, u32[]{:S(2)}) copy-start(f32[2,1,128]{2,1,0:T(1,128)} %get-tuple-element.5) | copy-start | bytes 3076

commit v2 on v1

--- a/solution.py
+++ b/solution.py
@@ -114,13 +114,12 @@
     load.wait()
 
     for i in range(count):
-        for p in range(2):
-            at = (2 * i + p) * COMPS
-            wide[at : at + COMPS, :] = raw[i, p].astype(jnp.float32)
+        at = 2 * COMPS * i
+        wide[at : at + 2 * COMPS, :] = raw[i].astype(jnp.float32).reshape(2 * COMPS, LANES)
     for a in range(SPINS):
         for p in range(2):
             for c in range(COLOURS):
-                rows = wide[pl.ds(p * COMPS + COLOURS * a + c, count, stride=2 * COMPS), :]
+                rows = wide[pl.ds(2 * (COLOURS * a + c) + p, count, stride=2 * COMPS), :]
                 at = (2 * a + p) * count
                 stack[at : at + count, c * LANES : (c + 1) * LANES] = rows.astype(jnp.bfloat16)
     everything = stack[...]
@@ -248,7 +247,10 @@
             rotated = pltpu.roll(held, count, 1) * turn
             out = jnp.where(anti, rotated, held)
             gram_ref[when, k * count : (k + 1) * count, :] = out * gram_scale
-            loops_ref[when, k : k + 1, :] = summed[k, half : half + 1] * loop_scale
+            sums = summed[k, half : half + 1] * loop_scale
+            at = slice(k * count, (k + 1) * count)
+            loops_ref[when, 0:1, at] = sums[:, :count]
+            loops_ref[when, 1:2, at] = pltpu.roll(sums, count, 1)[:, :count]
 
     unpack(total, time)
     for step in range(1, groups):
@@ -272,7 +274,7 @@
         ),
         out_shape=(
             jax.ShapeDtypeStruct((groups, per_owner * count, 2 * count), jnp.float32),
-            jax.ShapeDtypeStruct((groups, per_owner, 2 * count), jnp.float32),
+            jax.ShapeDtypeStruct((groups, 2, per_owner * count), jnp.float32),
         ),
         in_specs=[
             pl.BlockSpec(memory_space=pltpu.SMEM),
@@ -284,7 +286,7 @@
             pl.BlockSpec(memory_space=pltpu.VMEM),
         ),
         scratch_shapes=[
-            pltpu.VMEM((count, halves, comps, sites), jnp.bfloat16),
+            pltpu.VMEM((count, comps, halves, sites), jnp.bfloat16),
             pltpu.VMEM((count * halves * comps, sites), jnp.float32),
             pltpu.VMEM((SPINS * 2 * count, COLOURS * sites), jnp.bfloat16),
             pltpu.VMEM((SPINS * 2 * count, SPINS * 2 * count), jnp.float32),
@@ -300,9 +302,8 @@
             pltpu.SemaphoreType.DMA((groups - 1,)),
         ],
         compiler_params=pltpu.CompilerParams(collective_id=0, has_side_effects=True),
-    )(gamma_ids, dilution.reshape(1, count), vectors.reshape(count, halves, comps, sites))
-    loops = loops.reshape(groups, per_owner, 2, count).swapaxes(2, 3)
-    return gram, loops.reshape(groups, per_owner * count, 2)
+    )(gamma_ids, dilution.reshape(1, count), vectors.reshape(count, halves, comps, sites).swapaxes(1, 2))
+    return gram, loops.swapaxes(1, 2)
 
 
 def any_shards(vectors, dilution, gamma_ids):

time: 20.9 us -> 17.7 us (0.85)
  local copies, waits for them, and re-layouts: 4.65 us -> 2.06 us
  other arithmetic: 0.66 us -> 0 us
    unnamed x4, local copies, waits for them, and re-layouts: 3.48 us -> 2.06 us
    pallas_call x1 -> x0, other arithmetic: 0.66 us -> none  [packed_shards(): pl.pallas_call(partial(kernel, owners, groups, per_owner, 1.0 / math.sqrt...]
    reshape x1 -> x0, local copies, waits for them, and re-layouts: 0.66 us -> none  [packed_shards(): loops = loops.reshape(groups, per_owner, 2, count).swapaxes(2, 3)]
    pallas_call x1 -> x0, local copies, waits for them, and re-layouts: 0.51 us -> none  [packed_shards(): pl.pallas_call(partial(kernel, owners, groups, per_owner, 1.0 / math.sqrt...]
where the time goes in v2:
time: 17.7 us; the launch traced here: 17.5 us
  Pallas kernels  14.8 us (84%)
  local copies, waits for them, and re-layouts  2.06 us (12%)
  between operations  0.65 us (4%)
    pallas_call x1, Pallas kernels, packed_shards(): pl.pallas_call(partial(kernel, owners, groups, per_owner, 1.0 / math.sqrt...  14.8 us
    unnamed x4, local copies, waits for them, and re-layouts  2.06 us

profile of v2, /device:TPU:1, one launch (start us, length us, event | category | flops | bytes accessed | tf_op | source)
XLA Modules:
  0.0 17.5 jit_solution(11853508139927088312)
XLA Ops:
  0.6 14.8 %shard_map.50 = (f32[2,64,128]{2,1,0:T(8,128)}, f32[2,2,64]{2,1,0:T(2,128)}) custom-call(s32[16]{0:T(128)} %ids_ref.1, s32[1,64]{1,0:T(1,128)} %bitcast.7, bf16[64,12,2,128]{3,2,1,0:T(2,128)(2,1)} %bitcast.5), custom_call_target="tpu_custom_call" | custom-call | tf_op jit(solution)/shard_map/pallas_call | solution.py:270
  15.4 0.0 copy-start
  15.4 1.5 %copy.7 = f32[2,64,128]{2,1,0:T(8,128)} copy(f32[2,64,128]{2,1,0:T(8,128)} %get-tuple-element.8) | data formatting | bytes 131072
  16.9 0.0 copy-done
  16.9 0.6 %copy.8 = f32[2,64,2]{1,2,0:T(2,128)} copy(f32[2,64,2]{1,2,0:T(2,128)S(1)} %bitcast.6) | data formatting | bytes 2048
Async XLA Ops:
  15.4 1.5 %copy-start = (f32[2,2,64]{2,1,0:T(2,128)S(1)}, f32[2,2,64]{2,1,0:T(2,128)}, u32[]{:S(2)}) copy-start(f32[2,2,64]{2,1,0:T(2,128)} %get-tuple-element.5) | copy-start | bytes 3076

commit v3 on v2

--- a/solution.py
+++ b/solution.py
@@ -90,28 +90,50 @@
     return out
 
 
+def plane_of(owners):
+    return math.gcd(owners, 4)
+
+
 def kernel(
     owners, groups, per_owner, gram_scale, loop_scale,
-    ids_ref, dil_ref, vec_ref, gram_ref, loops_ref,
-    raw, wide, stack, pairs, packed, sendbuf, recvbuf, mine, theirs,
-    load_sem, send_sem, recv_sem, swap_send, swap_recv,
+    ids_hbm, dil_hbm, vec_ref, gram_ref, loops_ref,
+    ids_ref, dil_ref, raw, wide, stack, pairs, packed, sendbuf, recvbuf, midbuf, lastbuf,
+    mine, theirs,
+    load_sems, send_sem, recv_sem, mid_send, mid_recv, swap_send, swap_recv,
 ):
     count = vec_ref.shape[0]
     half = count // 2
     space = lax.axis_index("space")
     time = lax.axis_index("tm")
-    load = pltpu.make_async_copy(vec_ref, raw, load_sem)
-    load.start()
+    plane = plane_of(owners)
+    planes = owners // plane
+    place = lax.rem(space, plane)
+    level = lax.div(space, plane)
+    loads = [
+        pltpu.make_async_copy(vec_ref, raw, load_sems.at[0]),
+        pltpu.make_async_copy(ids_hbm, ids_ref, load_sems.at[1]),
+        pltpu.make_async_copy(dil_hbm, dil_ref, load_sems.at[2]),
+    ]
+    for load in loads:
+        load.start()
     barrier = pltpu.get_barrier_semaphore()
-    for step in range(1, owners):
-        pl.semaphore_signal(
-            barrier, inc=1, device_id=(lax.rem(space + step, owners), time), device_id_type=MESH
-        )
+    beside = [level * plane + lax.rem(place + step, plane) for step in range(1, plane)]
+    farther = []
+    for step in range(planes):
+        down = 2 * level >= planes
+        far = jnp.where(down, level, planes - 1 - level)
+        way = jnp.where(step < far, step, planes - 1 - (step - far))
+        way = jnp.where(step == planes - 1, far, way)
+        farther.append(jnp.where(down, way, planes - 1 - way))
+    along = [lax.rem(level + step, planes) * plane + place for step in range(1, planes)]
+    for target in beside + along:
+        pl.semaphore_signal(barrier, inc=1, device_id=(target, time), device_id_type=MESH)
     for step in range(1, groups):
         pl.semaphore_signal(
             barrier, inc=1, device_id=(space, lax.rem(time + step, groups)), device_id_type=MESH
         )
-    load.wait()
+    for load in loads:
+        load.wait()
 
     for i in range(count):
         at = 2 * COMPS * i
@@ -191,24 +213,54 @@
     for g in range(owners * per_owner):
         sendbuf[g] = packed[ids_ref[g]]
 
-    pl.semaphore_wait(barrier, owners + groups - 2)
+    pl.semaphore_wait(barrier, plane + planes + groups - 3)
     copies = []
-    for step in range(1, owners):
-        target = lax.rem(space + step, owners)
-        copy = pltpu.make_async_remote_copy(
-            src_ref=sendbuf.at[pl.ds(target * per_owner, per_owner)],
-            dst_ref=recvbuf.at[step - 1],
-            send_sem=send_sem.at[step - 1],
-            recv_sem=recv_sem.at[step - 1],
-            device_id=(target, time),
+    arrivals = []
+    for turn_no, target_level in enumerate(farther):
+        for step in range(1, plane):
+            target = beside[step - 1]
+            slot = turn_no * (plane - 1) + step - 1
+            goal = target_level * plane + lax.rem(place + step, plane)
+            copy = pltpu.make_async_remote_copy(
+                src_ref=sendbuf.at[pl.ds(goal * per_owner, per_owner)],
+                dst_ref=recvbuf.at[slot],
+                send_sem=send_sem.at[slot],
+                recv_sem=recv_sem.at[slot],
+                device_id=(target, time),
+                device_id_type=MESH,
+            )
+            copy.start()
+            copies.append(copy)
+            arrivals.append(copy)
+    for turn_no, target_level in enumerate(farther):
+        total = sendbuf[pl.ds((target_level * plane + place) * per_owner, per_owner)]
+        for step in range(1, plane):
+            slot = turn_no * (plane - 1) + step - 1
+            arrivals[slot].wait_recv()
+            total = total + recvbuf[slot]
+        if turn_no < planes - 1:
+            midbuf[turn_no] = total
+            slot = lax.rem(target_level - level + planes, planes) - 1
+            copy = pltpu.make_async_remote_copy(
+                src_ref=midbuf.at[turn_no],
+                dst_ref=lastbuf.at[slot],
+                send_sem=mid_send.at[turn_no],
+                recv_sem=mid_recv.at[slot],
+                device_id=(target_level * plane + place, time),
+                device_id_type=MESH,
+            )
+            copy.start()
+            copies.append(copy)
+    for slot in range(planes - 1):
+        pltpu.make_async_remote_copy(
+            src_ref=midbuf.at[slot],
+            dst_ref=lastbuf.at[slot],
+            send_sem=mid_send.at[slot],
+            recv_sem=mid_recv.at[slot],
+            device_id=(along[slot], time),
             device_id_type=MESH,
-        )
-        copy.start()
-        copies.append(copy)
-    total = sendbuf[pl.ds(space * per_owner, per_owner)]
-    for step in range(1, owners):
-        copies[step - 1].wait_recv()
-        total = total + recvbuf[step - 1]
+        ).wait_recv()
+        total = total + lastbuf[slot]
     mine[...] = total
     swaps = []
     for step in range(1, groups):
@@ -266,6 +318,8 @@
     numbers = gamma_ids.shape[0]
     per_owner = numbers // owners
     total_sites = sites * owners
+    plane = plane_of(owners)
+    planes = owners // plane
     message = (per_owner, count // 2 + 1, 2 * count)
     gram, loops = pl.pallas_call(
         partial(
@@ -277,8 +331,8 @@
             jax.ShapeDtypeStruct((groups, 2, per_owner * count), jnp.float32),
         ),
         in_specs=[
-            pl.BlockSpec(memory_space=pltpu.SMEM),
-            pl.BlockSpec(memory_space=pltpu.VMEM),
+            pl.BlockSpec(memory_space=pl.ANY),
+            pl.BlockSpec(memory_space=pl.ANY),
             pl.BlockSpec(memory_space=pl.ANY),
         ],
         out_specs=(
@@ -286,18 +340,24 @@
             pl.BlockSpec(memory_space=pltpu.VMEM),
         ),
         scratch_shapes=[
+            pltpu.SMEM((numbers,), jnp.int32),
+            pltpu.VMEM((1, count), jnp.int32),
             pltpu.VMEM((count, comps, halves, sites), jnp.bfloat16),
             pltpu.VMEM((count * halves * comps, sites), jnp.float32),
             pltpu.VMEM((SPINS * 2 * count, COLOURS * sites), jnp.bfloat16),
             pltpu.VMEM((SPINS * 2 * count, SPINS * 2 * count), jnp.float32),
             pltpu.VMEM((16,) + message[1:], jnp.float32),
             pltpu.VMEM((numbers,) + message[1:], jnp.float32),
-            pltpu.VMEM((owners - 1,) + message, jnp.float32),
+            pltpu.VMEM((planes * (plane - 1),) + message, jnp.float32),
+            pltpu.VMEM((planes - 1,) + message, jnp.float32),
+            pltpu.VMEM((planes - 1,) + message, jnp.float32),
             pltpu.VMEM(message, jnp.float32),
             pltpu.VMEM((groups - 1,) + message, jnp.float32),
-            pltpu.SemaphoreType.DMA,
-            pltpu.SemaphoreType.DMA((owners - 1,)),
-            pltpu.SemaphoreType.DMA((owners - 1,)),
+            pltpu.SemaphoreType.DMA((3,)),
+            pltpu.SemaphoreType.DMA((planes * (plane - 1),)),
+            pltpu.SemaphoreType.DMA((planes * (plane - 1),)),
+            pltpu.SemaphoreType.DMA((planes - 1,)),
+            pltpu.SemaphoreType.DMA((planes - 1,)),
             pltpu.SemaphoreType.DMA((groups - 1,)),
             pltpu.SemaphoreType.DMA((groups - 1,)),
         ],
@@ -309,7 +369,8 @@
 def any_shards(vectors, dilution, gamma_ids):
     slices, count, halves, comps, sites = vectors.shape
     numbers = gamma_ids.shape[0]
-    whole_blocks = numbers % lax.axis_size("space") == 0
+    owners, groups = lax.axis_size("space"), lax.axis_size("tm")
+    whole_blocks = numbers % owners == 0 and owners > plane_of(owners) > 1 and groups > 1
     if slices == 1 and sites == LANES and 2 * count == LANES and whole_blocks:
         return packed_shards(vectors, dilution, gamma_ids)
     return shards(vectors, dilution, gamma_ids)

time: 17.7 us -> 18.1 us (1.023)
  Pallas kernels: 14.8 us -> 15.2 us
    pallas_call x1, Pallas kernels: 14.8 us -> 15.2 us  [packed_shards(): pl.pallas_call(partial(kernel, owners, groups, per_owner, 1.0 / math.sqrt...]
where the time goes in v3:
time: 18.1 us; the launch traced here: 17.9 us
  Pallas kernels  15.2 us (84%)
  local copies, waits for them, and re-layouts  2.06 us (11%)
  between operations  0.65 us (4%)
    pallas_call x1, Pallas kernels, packed_shards(): pl.pallas_call(partial(kernel, owners, groups, per_owner, 1.0 / math.sqrt...  15.2 us
    unnamed x4, local copies, waits for them, and re-layouts  2.06 us

profile of v3, /device:TPU:1, one launch (start us, length us, event | category | flops | bytes accessed | tf_op | source)
XLA Modules:
  0.0 17.9 jit_solution(12475882619899103284)
XLA Ops:
  0.6 15.2 %shard_map.50 = (f32[2,64,128]{2,1,0:T(8,128)}, f32[2,2,64]{2,1,0:T(2,128)}) custom-call(s32[16]{0:T(128)} %ids_hbm.1, s32[1,64]{1,0:T(1,128)} %bitcast.7, bf16[64,12,2,128]{3,2,1,0:T(2,128)(2,1)} %bitcast.5), custom_call_target="tpu_custom_call" | custom-call | tf_op jit(solution)/shard_map/pallas_call | solution.py:324
  15.8 0.0 copy-start
  15.8 1.5 %copy.7 = f32[2,64,128]{2,1,0:T(8,128)} copy(f32[2,64,128]{2,1,0:T(8,128)} %get-tuple-element.8) | data formatting | bytes 131072
  17.3 0.0 copy-done
  17.3 0.6 %copy.8 = f32[2,64,2]{1,2,0:T(2,128)} copy(f32[2,64,2]{1,2,0:T(2,128)S(1)} %bitcast.6) | data formatting | bytes 2048
Async XLA Ops:
  15.8 1.5 %copy-start = (f32[2,2,64]{2,1,0:T(2,128)S(1)}, f32[2,2,64]{2,1,0:T(2,128)}, u32[]{:S(2)}) copy-start(f32[2,2,64]{2,1,0:T(2,128)} %get-tuple-element.5) | copy-start | bytes 3076

commit v4 on v2

--- a/solution.py
+++ b/solution.py
@@ -92,26 +92,32 @@
 
 def kernel(
     owners, groups, per_owner, gram_scale, loop_scale,
-    ids_ref, dil_ref, vec_ref, gram_ref, loops_ref,
-    raw, wide, stack, pairs, packed, sendbuf, recvbuf, mine, theirs,
-    load_sem, send_sem, recv_sem, swap_send, swap_recv,
+    ids_hbm, dil_hbm, vec_ref, gram_ref, loops_ref,
+    ids_ref, dil_ref, raw, wide, stack, pairs, packed, sendbuf, recvbuf,
+    mine, theirs,
+    load_sems, send_sem, recv_sem, swap_send, swap_recv,
 ):
     count = vec_ref.shape[0]
     half = count // 2
     space = lax.axis_index("space")
     time = lax.axis_index("tm")
-    load = pltpu.make_async_copy(vec_ref, raw, load_sem)
-    load.start()
+    loads = [
+        pltpu.make_async_copy(vec_ref, raw, load_sems.at[0]),
+        pltpu.make_async_copy(ids_hbm, ids_ref, load_sems.at[1]),
+        pltpu.make_async_copy(dil_hbm, dil_ref, load_sems.at[2]),
+    ]
+    for load in loads:
+        load.start()
     barrier = pltpu.get_barrier_semaphore()
-    for step in range(1, owners):
-        pl.semaphore_signal(
-            barrier, inc=1, device_id=(lax.rem(space + step, owners), time), device_id_type=MESH
-        )
+    targets = [lax.rem(space + step, owners) for step in range(1, owners)]
+    for target in targets:
+        pl.semaphore_signal(barrier, inc=1, device_id=(target, time), device_id_type=MESH)
     for step in range(1, groups):
         pl.semaphore_signal(
             barrier, inc=1, device_id=(space, lax.rem(time + step, groups)), device_id_type=MESH
         )
-    load.wait()
+    for load in loads:
+        load.wait()
 
     for i in range(count):
         at = 2 * COMPS * i
@@ -193,22 +199,21 @@
 
     pl.semaphore_wait(barrier, owners + groups - 2)
     copies = []
-    for step in range(1, owners):
-        target = lax.rem(space + step, owners)
+    for slot, target in enumerate(targets):
         copy = pltpu.make_async_remote_copy(
             src_ref=sendbuf.at[pl.ds(target * per_owner, per_owner)],
-            dst_ref=recvbuf.at[step - 1],
-            send_sem=send_sem.at[step - 1],
-            recv_sem=recv_sem.at[step - 1],
+            dst_ref=recvbuf.at[slot],
+            send_sem=send_sem.at[slot],
+            recv_sem=recv_sem.at[slot],
             device_id=(target, time),
             device_id_type=MESH,
         )
         copy.start()
         copies.append(copy)
     total = sendbuf[pl.ds(space * per_owner, per_owner)]
-    for step in range(1, owners):
-        copies[step - 1].wait_recv()
-        total = total + recvbuf[step - 1]
+    for slot in range(owners - 1):
+        copies[slot].wait_recv()
+        total = total + recvbuf[slot]
     mine[...] = total
     swaps = []
     for step in range(1, groups):
@@ -273,12 +278,12 @@
             1.0 / math.sqrt(48.0 * total_sites), 1.0 / math.sqrt(1.0 * total_sites),
         ),
         out_shape=(
-            jax.ShapeDtypeStruct((groups, per_owner * count, 2 * count), jnp.float32),
-            jax.ShapeDtypeStruct((groups, 2, per_owner * count), jnp.float32),
+            pltpu.VMEM((groups, per_owner * count, 2 * count), jnp.float32),
+            pltpu.VMEM((groups, 2, per_owner * count), jnp.float32),
         ),
         in_specs=[
-            pl.BlockSpec(memory_space=pltpu.SMEM),
-            pl.BlockSpec(memory_space=pltpu.VMEM),
+            pl.BlockSpec(memory_space=pl.ANY),
+            pl.BlockSpec(memory_space=pl.ANY),
             pl.BlockSpec(memory_space=pl.ANY),
         ],
         out_specs=(
@@ -286,6 +291,8 @@
             pl.BlockSpec(memory_space=pltpu.VMEM),
         ),
         scratch_shapes=[
+            pltpu.SMEM((numbers,), jnp.int32),
+            pltpu.VMEM((1, count), jnp.int32),
             pltpu.VMEM((count, comps, halves, sites), jnp.bfloat16),
             pltpu.VMEM((count * halves * comps, sites), jnp.float32),
             pltpu.VMEM((SPINS * 2 * count, COLOURS * sites), jnp.bfloat16),
@@ -295,7 +302,7 @@
             pltpu.VMEM((owners - 1,) + message, jnp.float32),
             pltpu.VMEM(message, jnp.float32),
             pltpu.VMEM((groups - 1,) + message, jnp.float32),
-            pltpu.SemaphoreType.DMA,
+            pltpu.SemaphoreType.DMA((3,)),
             pltpu.SemaphoreType.DMA((owners - 1,)),
             pltpu.SemaphoreType.DMA((owners - 1,)),
             pltpu.SemaphoreType.DMA((groups - 1,)),
@@ -309,7 +316,8 @@
 def any_shards(vectors, dilution, gamma_ids):
     slices, count, halves, comps, sites = vectors.shape
     numbers = gamma_ids.shape[0]
-    whole_blocks = numbers % lax.axis_size("space") == 0
+    owners, groups = lax.axis_size("space"), lax.axis_size("tm")
+    whole_blocks = numbers % owners == 0 and owners > 1 and groups > 1
     if slices == 1 and sites == LANES and 2 * count == LANES and whole_blocks:
         return packed_shards(vectors, dilution, gamma_ids)
     return shards(vectors, dilution, gamma_ids)

time: 17.7 us -> 15.5 us (0.88)
  Pallas kernels: 14.8 us -> 13.5 us
  local copies, waits for them, and re-layouts: 2.06 us -> 1.21 us
    pallas_call x1, Pallas kernels: 14.8 us -> 13.5 us  [packed_shards(): pl.pallas_call(partial(kernel, owners, groups, per_owner, 1.0 / math.sqrt...]
    unnamed x4 -> x2, local copies, waits for them, and re-layouts: 2.06 us -> 1.21 us
where the time goes in v4:
time: 15.5 us; the launch traced here: 15.3 us
  Pallas kernels  13.5 us (87%)
  local copies, waits for them, and re-layouts  1.21 us (8%)
  between operations  0.64 us (4%)
    pallas_call x1, Pallas kernels, packed_shards(): pl.pallas_call(partial(kernel, owners, groups, per_owner, 1.0 / math.sqrt...  13.5 us
    unnamed x2, local copies, waits for them, and re-layouts  1.21 us

profile of v4, /device:TPU:1, one launch (start us, length us, event | category | flops | bytes accessed | tf_op | source)
XLA Modules:
  0.0 15.3 jit_solution(5759291054525685096)
XLA Ops:
  0.6 13.5 %shard_map.50 = (f32[2,64,128]{2,1,0:T(8,128)S(1)}, f32[2,2,64]{2,1,0:T(2,128)S(1)}) custom-call(s32[16]{0:T(128)} %ids_hbm.1, s32[1,64]{1,0:T(1,128)} %bitcast.7, bf16[64,12,2,128]{3,2,1,0:T(2,128)(2,1)} %bitcast.6), custom_call_target="tpu_custom_call" | custom-call | tf_op jit(solution)/shard_map/pallas_call | solution.py:275
  14.1 0.6 %copy.7 = f32[2,64,128]{2,1,0:T(8,128)} copy(f32[2,64,128]{2,1,0:T(8,128)S(1)} %get-tuple-element.6) | data formatting | bytes 131072
  14.8 0.6 %copy.8 = f32[2,64,2]{1,2,0:T(2,128)} copy(f32[2,64,2]{1,2,0:T(2,128)S(1)} %bitcast.5) | data formatting | bytes 2048
